TPU v7x, 256 devices: a whole 4x4x8 slice. The times are simulated.
256 devices in a mesh: dp: 8 (over x, z_lo), section: 8 (over z_hi, core), tensor: 4 (over y).
Axes of the slice: x: 4, y: 4, z: 8 (z_hi: 4, z_lo: 2; z = z_hi * 2 + z_lo), core: 2. Of those that a mesh axis runs over, the one named last changes fastest.
Arguments:
- cotangent: bfloat16 [2, 64, 6144], P(None, 'tensor', 'dp'), may hold values from -6 to 6
- inputs: bfloat16 [8, 2, 64, 6144], P('section', None, 'tensor', 'dp'), may hold values from -6 to 6
- queries: bfloat16 [8, 2, 64, 6144], P('section', None, None, 'tensor'), may hold values from -256 to 256
- keys: bfloat16 [8, 2, 64, 6144], P('section', None, None, 'tensor'), may hold values from -8 to 8
- context: bfloat16 [8, 2, 64, 6144], P('section', None, None, 'tensor'), may hold values from -6 to 6
- value_weight: bfloat16 [8, 6144, 6144], P('section', 'dp', 'tensor'), may hold values from -0.078125 to 0.078125
- out_weight: bfloat16 [8, 6144, 6144], P('section', 'tensor', 'dp'), may hold values from -0.078125 to 0.078125
Outputs:
- section_grads: bfloat16 [8, 2, 64, 6144], P('section', None, 'tensor', 'dp')
- value_weight_grad: bfloat16 [8, 6144, 6144], P('section', 'dp', 'tensor')
- out_weight_grad: bfloat16 [8, 6144, 6144], P('section', 'tensor', 'dp')
All inputs are finite; a program needn't handle non-finite values.
Results may differ from a plain program's by a relative error of at most 0.018.
Values may be sent and summed in bfloat16 or wider, within the bound.
A program may use at most 64 MiB of HBM per device.

v0:
```python
import jax
import jax.numpy as jnp
from jax import lax
from jax.sharding import PartitionSpec as P

HEAD_DIM = 128


def copy_for_each(array, axis):
    copies = jnp.broadcast_to(array, (lax.axis_size(axis), *array.shape))
    return lax.all_to_all(copies, axis, split_axis=0, concat_axis=0, tiled=True)


def laid_out(tiles, dim):
    tiles = jnp.moveaxis(tiles, 0, dim)
    shape = tiles.shape
    return tiles.reshape(*shape[:dim], shape[dim] * shape[dim + 1], *shape[dim + 2 :])


def gather_directly(array, axis, dim):
    tiles = copy_for_each(array, axis)
    return laid_out(tiles, dim)


def in_blocks(array, dim, peers):
    shape = array.shape
    tiles = array.reshape(*shape[:dim], peers, shape[dim] // peers, *shape[dim + 1 :])
    return jnp.moveaxis(tiles, dim, 0)


def sum_at_owner(array, axis, dim):
    tiles = in_blocks(array, dim, lax.axis_size(axis))
    arrived = lax.all_to_all(tiles, axis, split_axis=0, concat_axis=0, tiled=True)
    return arrived.sum(axis=0)


def shifted(array, axis, by):
    peers = lax.axis_size(axis)
    pairs = [(i, i + by) for i in range(peers) if 0 <= i + by < peers]
    return lax.ppermute(array, axis, pairs)


def attention_probs(query_layer, key_layer):
    micro_count, seq_len, width = query_layer.shape
    head_count = width // HEAD_DIM
    query_heads = query_layer.reshape(micro_count, seq_len, head_count, HEAD_DIM)
    key_heads = key_layer.reshape(micro_count, seq_len, head_count, HEAD_DIM)
    scores = jnp.einsum(
        "mihd,mjhd->mhij", query_heads, key_heads, preferred_element_type=jnp.float32
    )
    scores = scores / jnp.sqrt(jnp.float32(HEAD_DIM))
    rows = jnp.arange(seq_len)
    causal = rows[:, None] >= rows[None, :]
    scores = jnp.where(causal[None, None], scores, jnp.float32(-1e30))
    highest = jnp.max(scores, axis=-1, keepdims=True)
    expo = jnp.exp(scores - highest)
    return (expo / jnp.sum(expo, axis=-1, keepdims=True)).astype(jnp.bfloat16)


def per_device(cotangent, inputs, queries, keys, context, value_weight, out_weight):
    section_count = lax.axis_size("section")
    dp_count = lax.axis_size("dp")
    section_place = lax.axis_index("section")
    micro_count = cotangent.shape[0]
    part_rows = cotangent.shape[1]
    width_cols = cotangent.shape[2]
    head_cols = queries.shape[3]
    heads_here = head_cols // HEAD_DIM
    value_proj = value_weight[0]
    out_proj = out_weight[0]
    saved_context = context[0]
    whole_inputs = gather_directly(inputs[0], "tensor", 1)
    attention = attention_probs(queries[0], keys[0])
    share_cols = head_cols // dp_count
    col_start = lax.axis_index("dp") * share_cols
    col_heads = (col_start + jnp.arange(share_cols)) // HEAD_DIM
    head_mask = (jnp.arange(heads_here)[:, None] == col_heads[None, :]).astype(jnp.bfloat16)

    def tick(tick_number, carry):
        received, acc_out, acc_value, grads = carry
        raw_index = tick_number - (section_count - 1 - section_place)
        valid = (raw_index >= 0) & (raw_index < micro_count)
        micro_index = jnp.clip(raw_index, 0, micro_count - 1)
        cot_here = lax.dynamic_index_in_dim(cotangent, micro_index, 0, keepdims=False)
        incoming = jnp.where(section_place == section_count - 1, cot_here, received)
        grad_cols = gather_directly(incoming, "tensor", 0)
        ctx_part = lax.dot_general(
            grad_cols, out_proj, (((1,), (1,)), ((), ())), preferred_element_type=jnp.float32
        )
        attn_here = lax.dynamic_index_in_dim(attention, micro_index, 0, keepdims=False)
        ctx_share = sum_at_owner(ctx_part, "dp", 1).astype(jnp.bfloat16)
        masked = ctx_share[None, :, :] * head_mask[:, None, :]
        value_share = jnp.einsum(
            "hij,hic->jc", attn_here, masked, preferred_element_type=jnp.float32
        )
        value_grad = gather_directly(value_share.astype(jnp.bfloat16), "dp", 1)
        input_here = lax.dynamic_index_in_dim(whole_inputs, micro_index, 0, keepdims=False)
        context_here = lax.dynamic_index_in_dim(saved_context, micro_index, 0, keepdims=False)
        value_term = lax.dot_general(
            input_here, value_grad, (((0,), (0,)), ((), ())), preferred_element_type=jnp.float32
        )
        out_term = lax.dot_general(
            context_here, grad_cols, (((0,), (0,)), ((), ())), preferred_element_type=jnp.float32
        )
        acc_value = acc_value + jnp.where(valid, value_term, jnp.float32(0.0))
        acc_out = acc_out + jnp.where(valid, out_term, jnp.float32(0.0))
        branch = lax.dot_general(
            value_grad, value_proj, (((1,), (1,)), ((), ())), preferred_element_type=jnp.float32
        )
        summed = sum_at_owner(branch, "tensor", 0)
        fresh = (summed + incoming.astype(jnp.float32)).astype(jnp.bfloat16)
        passed = shifted(fresh, "section", -1)
        current = lax.dynamic_index_in_dim(grads, micro_index, 0, keepdims=False)
        grads = lax.dynamic_update_index_in_dim(
            grads, jnp.where(valid, fresh, current), micro_index, 0
        )
        return (passed, acc_out, acc_value, grads)

    start_recv = jnp.zeros((part_rows, width_cols), jnp.bfloat16)
    start_out = jnp.zeros((head_cols, width_cols), jnp.float32)
    start_value = jnp.zeros((width_cols, head_cols), jnp.float32)
    start_grads = jnp.zeros((micro_count, part_rows, width_cols), jnp.bfloat16)
    final = lax.fori_loop(
        0, micro_count + section_count - 1, tick, (start_recv, start_out, start_value, start_grads)
    )
    acc_out = final[1]
    acc_value = final[2]
    grads = final[3]
    return (grads[None], acc_value.astype(jnp.bfloat16)[None], acc_out.astype(jnp.bfloat16)[None])


def solution(mesh):
    placed = (
        P(None, "tensor", "dp"),
        P("section", None, "tensor", "dp"),
        P("section", None, None, "tensor"),
        P("section", None, None, "tensor"),
        P("section", None, None, "tensor"),
        P("section", "dp", "tensor"),
        P("section", "tensor", "dp"),
    )
    return jax.shard_map(
        per_device,
        mesh=mesh,
        in_specs=placed,
        out_specs=(
            P("section", None, "tensor", "dp"),
            P("section", "dp", "tensor"),
            P("section", "tensor", "dp"),
        ),
        check_vma=False,
    )
```

profile of v0, /device:TPU:2, one launch (start us, length us, event | category | flops | bytes accessed | tf_op | source)
XLA Modules:
  0.0 553.7 jit_solution(9358829543437963657)
XLA Ops:
  17.1 530.7 %while.22 = (s32[]{:T(128)}, bf16[16,768]{1,0:T(8,128)(2,1)S(1)}, f32[1536,768]{1,0:T(8,128)}, f32[768,1536]{1,0:T(8,128)}, bf16[2,16,768]{2,1,0:T(8,128)(2,1)S(...) while((s32[]{:T(128)}, bf16[16,768]{1,0:T(8,128)(2,1)S(1)}, ...), condition=%wide.region_5.6_spmd.clone, body=%wide.region_2.5_spmd.clone.sunk | while | flops 630280704 | bytes 31228172 | solution.py:123
  18.0 8.2 %all_to_all.57 = bf16[4,16,768]{2,1,0:T(8,128)(2,1)S(1)} all-to-all(bf16[4,16,768]{2,1,0:T(8,128)(2,1)S(1)} %broadcast_in_dim.124), channel_id=1, replica_groups=mesh['dp'=8,'section'=8,'tensor'=4] {'tensor'}, dimensions={0} | all-to-all | bytes 196608 | tf_op jit(solution)/shard_map/while/body/eval_jaxpr/all_to_all | solution.py:11
  27.8 6.2 %all-to-all-start.1 = ((f32[8,64,192]{2,1,0:T(8,128)}), f32[8,64,192]{2,1,0:T(8,128)S(1)}, u32[]{:S(2)}, u32[]{:S(2)}) async-start(f32[8,64,192]{2,1,0:T(8,128)} %convolution_bitcast_fusion.3), calls=%async_computation.1 | async-start | bytes 1048576 | tf_op jit(solution)/shard_map/while/body/eval_jaxpr/all_to_all | solution.py:33
  34.0 6.8 %all-to-all-done.1 = f32[8,64,192]{2,1,0:T(8,128)S(1)} async-done(((f32[8,64,192]{2,1,0:T(8,128)}), f32[8,64,192]{2,1,0:T(8,128)S(1)}, u32[]{:S(2)}, u32[]{:S(2)}) %all-to-all-start.1) | async-done | bytes 393248 | tf_op jit(solution)/shard_map/while/body/eval_jaxpr/all_to_all | solution.py:33
  47.9 5.5 all-to-all-done.2
  73.3 8.2 %all_to_all.57 = bf16[4,16,768]{2,1,0:T(8,128)(2,1)S(1)} all-to-all(bf16[4,16,768]{2,1,0:T(8,128)(2,1)S(1)} %broadcast_in_dim.124), channel_id=1, replica_groups=mesh['dp'=8,'section'=8,'tensor'=4] {'tensor'}, dimensions={0} | all-to-all | bytes 196608 | tf_op jit(solution)/shard_map/while/body/eval_jaxpr/all_to_all | solution.py:11
  88.4 8.9 %all-to-all-done.1 = f32[8,64,192]{2,1,0:T(8,128)S(1)} async-done(((f32[8,64,192]{2,1,0:T(8,128)}), f32[8,64,192]{2,1,0:T(8,128)S(1)}, u32[]{:S(2)}, u32[]{:S(2)}) %all-to-all-start.1) | async-done | bytes 393248 | tf_op jit(solution)/shard_map/while/body/eval_jaxpr/all_to_all | solution.py:33
  99.2 5.4 all-to-all-start.2
  104.7 5.8 %all-to-all-done.2 = bf16[8,64,192]{2,1,0:T(8,128)(2,1)S(1)} async-done(((bf16[8,64,192]{2,1,0:T(8,128)(2,1)}), bf16[8,64,192]{2,1,0:T(8,128)(2,1)S(1)}, u32[]{:S(2)}, u32[]{:S(2)}) %all-to-all-start.2) | async-done | bytes 196640 | tf_op jit(solution)/shard_map/while/body/eval_jaxpr/all_to_all | solution.py:11
  131.8 10.0 %all_to_all.57 = bf16[4,16,768]{2,1,0:T(8,128)(2,1)S(1)} all-to-all(bf16[4,16,768]{2,1,0:T(8,128)(2,1)S(1)} %broadcast_in_dim.124), channel_id=1, replica_groups=mesh['dp'=8,'section'=8,'tensor'=4] {'tensor'}, dimensions={0} | all-to-all | bytes 196608 | tf_op jit(solution)/shard_map/while/body/eval_jaxpr/all_to_all | solution.py:11
  148.5 8.4 %all-to-all-done.1 = f32[8,64,192]{2,1,0:T(8,128)S(1)} async-done(((f32[8,64,192]{2,1,0:T(8,128)}), f32[8,64,192]{2,1,0:T(8,128)S(1)}, u32[]{:S(2)}, u32[]{:S(2)}) %all-to-all-start.1) | async-done | bytes 393248 | tf_op jit(solution)/shard_map/while/body/eval_jaxpr/all_to_all | solution.py:33
  158.8 5.4 all-to-all-start.2
  164.3 5.5 all-to-all-done.2
  191.2 10.0 %all_to_all.57 = bf16[4,16,768]{2,1,0:T(8,128)(2,1)S(1)} all-to-all(bf16[4,16,768]{2,1,0:T(8,128)(2,1)S(1)} %broadcast_in_dim.124), channel_id=1, replica_groups=mesh['dp'=8,'section'=8,'tensor'=4] {'tensor'}, dimensions={0} | all-to-all | bytes 196608 | tf_op jit(solution)/shard_map/while/body/eval_jaxpr/all_to_all | solution.py:11
  208.0 8.4 %all-to-all-done.1 = f32[8,64,192]{2,1,0:T(8,128)S(1)} async-done(((f32[8,64,192]{2,1,0:T(8,128)}), f32[8,64,192]{2,1,0:T(8,128)S(1)}, u32[]{:S(2)}, u32[]{:S(2)}) %all-to-all-start.1) | async-done | bytes 393248 | tf_op jit(solution)/shard_map/while/body/eval_jaxpr/all_to_all | solution.py:33
  223.8 5.5 all-to-all-done.2
  250.7 10.0 %all_to_all.57 = bf16[4,16,768]{2,1,0:T(8,128)(2,1)S(1)} all-to-all(bf16[4,16,768]{2,1,0:T(8,128)(2,1)S(1)} %broadcast_in_dim.124), channel_id=1, replica_groups=mesh['dp'=8,'section'=8,'tensor'=4] {'tensor'}, dimensions={0} | all-to-all | bytes 196608 | tf_op jit(solution)/shard_map/while/body/eval_jaxpr/all_to_all | solution.py:11
  267.6 8.4 %all-to-all-done.1 = f32[8,64,192]{2,1,0:T(8,128)S(1)} async-done(((f32[8,64,192]{2,1,0:T(8,128)}), f32[8,64,192]{2,1,0:T(8,128)S(1)}, u32[]{:S(2)}, u32[]{:S(2)}) %all-to-all-start.1) | async-done | bytes 393248 | tf_op jit(solution)/shard_map/while/body/eval_jaxpr/all_to_all | solution.py:33
  283.4 5.5 all-to-all-done.2
  310.3 10.0 %all_to_all.57 = bf16[4,16,768]{2,1,0:T(8,128)(2,1)S(1)} all-to-all(bf16[4,16,768]{2,1,0:T(8,128)(2,1)S(1)} %broadcast_in_dim.124), channel_id=1, replica_groups=mesh['dp'=8,'section'=8,'tensor'=4] {'tensor'}, dimensions={0} | all-to-all | bytes 196608 | tf_op jit(solution)/shard_map/while/body/eval_jaxpr/all_to_all | solution.py:11
  327.2 8.4 %all-to-all-done.1 = f32[8,64,192]{2,1,0:T(8,128)S(1)} async-done(((f32[8,64,192]{2,1,0:T(8,128)}), f32[8,64,192]{2,1,0:T(8,128)S(1)}, u32[]{:S(2)}, u32[]{:S(2)}) %all-to-all-start.1) | async-done | bytes 393248 | tf_op jit(solution)/shard_map/while/body/eval_jaxpr/all_to_all | solution.py:33
  337.6 5.4 all-to-all-start.2
  343.0 5.5 all-to-all-done.2
  369.9 10.0 %all_to_all.57 = bf16[4,16,768]{2,1,0:T(8,128)(2,1)S(1)} all-to-all(bf16[4,16,768]{2,1,0:T(8,128)(2,1)S(1)} %broadcast_in_dim.124), channel_id=1, replica_groups=mesh['dp'=8,'section'=8,'tensor'=4] {'tensor'}, dimensions={0} | all-to-all | bytes 196608 | tf_op jit(solution)/shard_map/while/body/eval_jaxpr/all_to_all | solution.py:11
  386.8 8.4 %all-to-all-done.1 = f32[8,64,192]{2,1,0:T(8,128)S(1)} async-done(((f32[8,64,192]{2,1,0:T(8,128)}), f32[8,64,192]{2,1,0:T(8,128)S(1)}, u32[]{:S(2)}, u32[]{:S(2)}) %all-to-all-start.1) | async-done | bytes 393248 | tf_op jit(solution)/shard_map/while/body/eval_jaxpr/all_to_all | solution.py:33
  402.6 5.5 all-to-all-done.2
  429.5 10.0 %all_to_all.57 = bf16[4,16,768]{2,1,0:T(8,128)(2,1)S(1)} all-to-all(bf16[4,16,768]{2,1,0:T(8,128)(2,1)S(1)} %broadcast_in_dim.124), channel_id=1, replica_groups=mesh['dp'=8,'section'=8,'tensor'=4] {'tensor'}, dimensions={0} | all-to-all | bytes 196608 | tf_op jit(solution)/shard_map/while/body/eval_jaxpr/all_to_all | solution.py:11
  446.4 8.4 %all-to-all-done.1 = f32[8,64,192]{2,1,0:T(8,128)S(1)} async-done(((f32[8,64,192]{2,1,0:T(8,128)}), f32[8,64,192]{2,1,0:T(8,128)S(1)}, u32[]{:S(2)}, u32[]{:S(2)}) %all-to-all-start.1) | async-done | bytes 393248 | tf_op jit(solution)/shard_map/while/body/eval_jaxpr/all_to_all | solution.py:33
  462.2 5.5 all-to-all-done.2
  489.1 10.0 %all_to_all.57 = bf16[4,16,768]{2,1,0:T(8,128)(2,1)S(1)} all-to-all(bf16[4,16,768]{2,1,0:T(8,128)(2,1)S(1)} %broadcast_in_dim.124), channel_id=1, replica_groups=mesh['dp'=8,'section'=8,'tensor'=4] {'tensor'}, dimensions={0} | all-to-all | bytes 196608 | tf_op jit(solution)/shard_map/while/body/eval_jaxpr/all_to_all | solution.py:11
  505.9 8.4 %all-to-all-done.1 = f32[8,64,192]{2,1,0:T(8,128)S(1)} async-done(((f32[8,64,192]{2,1,0:T(8,128)}), f32[8,64,192]{2,1,0:T(8,128)S(1)}, u32[]{:S(2)}, u32[]{:S(2)}) %all-to-all-start.1) | async-done | bytes 393248 | tf_op jit(solution)/shard_map/while/body/eval_jaxpr/all_to_all | solution.py:33
  521.7 5.5 all-to-all-done.2
  (289 shorter events, 318.2 us)
Async XLA Ops:
  5.6 10.8 %all-to-all-start.4 = ((bf16[4,2,16,768]{3,2,1,0:T(8,128)(2,1)}), bf16[4,2,16,768]{3,2,1,0:T(8,128)(2,1)S(1)}, u32[]{:S(2)}, u32[]{:S(2)}) async-start(bf16[4,2,16,768]{3,2,1,0:T(8,128)(2,1)} %broadcast_in_dim.103), calls=%async_computation.4 | async-start | bytes 393216 | tf_op jit(solution)/shard_map/all_to_all | solution.py:11
  27.8 13.0 %all-to-all-start.1 = ((f32[8,64,192]{2,1,0:T(8,128)}), f32[8,64,192]{2,1,0:T(8,128)S(1)}, u32[]{:S(2)}, u32[]{:S(2)}) async-start(f32[8,64,192]{2,1,0:T(8,128)} %convolution_bitcast_fusion.3), calls=%async_computation.1 | async-start | bytes 1048576 | tf_op jit(solution)/shard_map/while/body/eval_jaxpr/all_to_all | solution.py:33
  42.7 10.7 %all-to-all-start.2 = ((bf16[8,64,192]{2,1,0:T(8,128)(2,1)}), bf16[8,64,192]{2,1,0:T(8,128)(2,1)S(1)}, u32[]{:S(2)}, u32[]{:S(2)}) async-start(bf16[8,64,192]{2,1,0:T(8,128)(2,1)} %broadcast_in_dim.125), calls=%async_computation.2 | async-start | bytes 524288 | tf_op jit(solution)/shard_map/while/body/eval_jaxpr/all_to_all | solution.py:11
  57.0 9.7 %all-to-all-start.3 = ((f32[4,16,768]{2,1,0:T(8,128)}), f32[4,16,768]{2,1,0:T(8,128)S(1)}, u32[]{:S(2)}, u32[]{:S(2)}) async-start(f32[4,16,768]{2,1,0:T(8,128)} %fusion.66), calls=%async_computation.3 | async-start | bytes 393216 | tf_op jit(solution)/shard_map/while/body/eval_jaxpr/all_to_all | solution.py:33
  83.2 14.1 %all-to-all-start.1 = ((f32[8,64,192]{2,1,0:T(8,128)}), f32[8,64,192]{2,1,0:T(8,128)S(1)}, u32[]{:S(2)}, u32[]{:S(2)}) async-start(f32[8,64,192]{2,1,0:T(8,128)} %convolution_bitcast_fusion.3), calls=%async_computation.1 | async-start | bytes 1048576 | tf_op jit(solution)/shard_map/while/body/eval_jaxpr/all_to_all | solution.py:33
  99.2 11.2 %all-to-all-start.2 = ((bf16[8,64,192]{2,1,0:T(8,128)(2,1)}), bf16[8,64,192]{2,1,0:T(8,128)(2,1)S(1)}, u32[]{:S(2)}, u32[]{:S(2)}) async-start(bf16[8,64,192]{2,1,0:T(8,128)(2,1)} %broadcast_in_dim.125), calls=%async_computation.2 | async-start | bytes 524288 | tf_op jit(solution)/shard_map/while/body/eval_jaxpr/all_to_all | solution.py:11
  114.0 9.7 %all-to-all-start.3 = ((f32[4,16,768]{2,1,0:T(8,128)}), f32[4,16,768]{2,1,0:T(8,128)S(1)}, u32[]{:S(2)}, u32[]{:S(2)}) async-start(f32[4,16,768]{2,1,0:T(8,128)} %fusion.66), calls=%async_computation.3 | async-start | bytes 393216 | tf_op jit(solution)/shard_map/while/body/eval_jaxpr/all_to_all | solution.py:33
  124.3 6.7 %collective-permute-start = (bf16[16,768]{1,0:T(8,128)(2,1)S(1)}, bf16[16,768]{1,0:T(8,128)(2,1)S(1)}, u32[]{:S(2)}, u32[]{:S(2)}) collective-permute-start(bf16[16,768]{1,0:T(8,128)(2,1)S(1)} %get-tuple-element.474), channel_id=1, source_target_pairs={{4,0},{8,4},{12,8},{16,12},{20,16},{24,20},{28,24},{5,1},{9,5},{13... | collective-permute-start | bytes 73736 | tf_op jit(solution)/shard_map/while/body/eval_jaxpr/ppermute | solution.py:40
  143.5 13.4 %all-to-all-start.1 = ((f32[8,64,192]{2,1,0:T(8,128)}), f32[8,64,192]{2,1,0:T(8,128)S(1)}, u32[]{:S(2)}, u32[]{:S(2)}) async-start(f32[8,64,192]{2,1,0:T(8,128)} %convolution_bitcast_fusion.3), calls=%async_computation.1 | async-start | bytes 1048576 | tf_op jit(solution)/shard_map/while/body/eval_jaxpr/all_to_all | solution.py:33
  158.8 11.0 %all-to-all-start.2 = ((bf16[8,64,192]{2,1,0:T(8,128)(2,1)}), bf16[8,64,192]{2,1,0:T(8,128)(2,1)S(1)}, u32[]{:S(2)}, u32[]{:S(2)}) async-start(bf16[8,64,192]{2,1,0:T(8,128)(2,1)} %broadcast_in_dim.125), calls=%async_computation.2 | async-start | bytes 524288 | tf_op jit(solution)/shard_map/while/body/eval_jaxpr/all_to_all | solution.py:11
  173.3 9.7 %all-to-all-start.3 = ((f32[4,16,768]{2,1,0:T(8,128)}), f32[4,16,768]{2,1,0:T(8,128)S(1)}, u32[]{:S(2)}, u32[]{:S(2)}) async-start(f32[4,16,768]{2,1,0:T(8,128)} %fusion.66), calls=%async_computation.3 | async-start | bytes 393216 | tf_op jit(solution)/shard_map/while/body/eval_jaxpr/all_to_all | solution.py:33
  202.8 13.6 %all-to-all-start.1 = ((f32[8,64,192]{2,1,0:T(8,128)}), f32[8,64,192]{2,1,0:T(8,128)S(1)}, u32[]{:S(2)}, u32[]{:S(2)}) async-start(f32[8,64,192]{2,1,0:T(8,128)} %convolution_bitcast_fusion.3), calls=%async_computation.1 | async-start | bytes 1048576 | tf_op jit(solution)/shard_map/while/body/eval_jaxpr/all_to_all | solution.py:33
  218.4 11.0 %all-to-all-start.2 = ((bf16[8,64,192]{2,1,0:T(8,128)(2,1)}), bf16[8,64,192]{2,1,0:T(8,128)(2,1)S(1)}, u32[]{:S(2)}, u32[]{:S(2)}) async-start(bf16[8,64,192]{2,1,0:T(8,128)(2,1)} %broadcast_in_dim.125), calls=%async_computation.2 | async-start | bytes 524288 | tf_op jit(solution)/shard_map/while/body/eval_jaxpr/all_to_all | solution.py:11
  232.9 9.7 %all-to-all-start.3 = ((f32[4,16,768]{2,1,0:T(8,128)}), f32[4,16,768]{2,1,0:T(8,128)S(1)}, u32[]{:S(2)}, u32[]{:S(2)}) async-start(f32[4,16,768]{2,1,0:T(8,128)} %fusion.66), calls=%async_computation.3 | async-start | bytes 393216 | tf_op jit(solution)/shard_map/while/body/eval_jaxpr/all_to_all | solution.py:33
  243.2 6.7 %collective-permute-start = (bf16[16,768]{1,0:T(8,128)(2,1)S(1)}, bf16[16,768]{1,0:T(8,128)(2,1)S(1)}, u32[]{:S(2)}, u32[]{:S(2)}) collective-permute-start(bf16[16,768]{1,0:T(8,128)(2,1)S(1)} %get-tuple-element.474), channel_id=1, source_target_pairs={{4,0},{8,4},{12,8},{16,12},{20,16},{24,20},{28,24},{5,1},{9,5},{13... | collective-permute-start | bytes 73736 | tf_op jit(solution)/shard_map/while/body/eval_jaxpr/ppermute | solution.py:40
  262.4 13.6 %all-to-all-start.1 = ((f32[8,64,192]{2,1,0:T(8,128)}), f32[8,64,192]{2,1,0:T(8,128)S(1)}, u32[]{:S(2)}, u32[]{:S(2)}) async-start(f32[8,64,192]{2,1,0:T(8,128)} %convolution_bitcast_fusion.3), calls=%async_computation.1 | async-start | bytes 1048576 | tf_op jit(solution)/shard_map/while/body/eval_jaxpr/all_to_all | solution.py:33
  278.0 11.0 %all-to-all-start.2 = ((bf16[8,64,192]{2,1,0:T(8,128)(2,1)}), bf16[8,64,192]{2,1,0:T(8,128)(2,1)S(1)}, u32[]{:S(2)}, u32[]{:S(2)}) async-start(bf16[8,64,192]{2,1,0:T(8,128)(2,1)} %broadcast_in_dim.125), calls=%async_computation.2 | async-start | bytes 524288 | tf_op jit(solution)/shard_map/while/body/eval_jaxpr/all_to_all | solution.py:11
  292.5 9.7 %all-to-all-start.3 = ((f32[4,16,768]{2,1,0:T(8,128)}), f32[4,16,768]{2,1,0:T(8,128)S(1)}, u32[]{:S(2)}, u32[]{:S(2)}) async-start(f32[4,16,768]{2,1,0:T(8,128)} %fusion.66), calls=%async_computation.3 | async-start | bytes 393216 | tf_op jit(solution)/shard_map/while/body/eval_jaxpr/all_to_all | solution.py:33
  322.0 13.6 %all-to-all-start.1 = ((f32[8,64,192]{2,1,0:T(8,128)}), f32[8,64,192]{2,1,0:T(8,128)S(1)}, u32[]{:S(2)}, u32[]{:S(2)}) async-start(f32[8,64,192]{2,1,0:T(8,128)} %convolution_bitcast_fusion.3), calls=%async_computation.1 | async-start | bytes 1048576 | tf_op jit(solution)/shard_map/while/body/eval_jaxpr/all_to_all | solution.py:33
  337.6 11.0 %all-to-all-start.2 = ((bf16[8,64,192]{2,1,0:T(8,128)(2,1)}), bf16[8,64,192]{2,1,0:T(8,128)(2,1)S(1)}, u32[]{:S(2)}, u32[]{:S(2)}) async-start(bf16[8,64,192]{2,1,0:T(8,128)(2,1)} %broadcast_in_dim.125), calls=%async_computation.2 | async-start | bytes 524288 | tf_op jit(solution)/shard_map/while/body/eval_jaxpr/all_to_all | solution.py:11
  352.1 9.7 %all-to-all-start.3 = ((f32[4,16,768]{2,1,0:T(8,128)}), f32[4,16,768]{2,1,0:T(8,128)S(1)}, u32[]{:S(2)}, u32[]{:S(2)}) async-start(f32[4,16,768]{2,1,0:T(8,128)} %fusion.66), calls=%async_computation.3 | async-start | bytes 393216 | tf_op jit(solution)/shard_map/while/body/eval_jaxpr/all_to_all | solution.py:33
  362.4 6.7 %collective-permute-start = (bf16[16,768]{1,0:T(8,128)(2,1)S(1)}, bf16[16,768]{1,0:T(8,128)(2,1)S(1)}, u32[]{:S(2)}, u32[]{:S(2)}) collective-permute-start(bf16[16,768]{1,0:T(8,128)(2,1)S(1)} %get-tuple-element.474), channel_id=1, source_target_pairs={{4,0},{8,4},{12,8},{16,12},{20,16},{24,20},{28,24},{5,1},{9,5},{13... | collective-permute-start | bytes 73736 | tf_op jit(solution)/shard_map/while/body/eval_jaxpr/ppermute | solution.py:40
  381.6 13.6 %all-to-all-start.1 = ((f32[8,64,192]{2,1,0:T(8,128)}), f32[8,64,192]{2,1,0:T(8,128)S(1)}, u32[]{:S(2)}, u32[]{:S(2)}) async-start(f32[8,64,192]{2,1,0:T(8,128)} %convolution_bitcast_fusion.3), calls=%async_computation.1 | async-start | bytes 1048576 | tf_op jit(solution)/shard_map/while/body/eval_jaxpr/all_to_all | solution.py:33
  397.2 11.0 %all-to-all-start.2 = ((bf16[8,64,192]{2,1,0:T(8,128)(2,1)}), bf16[8,64,192]{2,1,0:T(8,128)(2,1)S(1)}, u32[]{:S(2)}, u32[]{:S(2)}) async-start(bf16[8,64,192]{2,1,0:T(8,128)(2,1)} %broadcast_in_dim.125), calls=%async_computation.2 | async-start | bytes 524288 | tf_op jit(solution)/shard_map/while/body/eval_jaxpr/all_to_all | solution.py:11
  411.7 9.7 %all-to-all-start.3 = ((f32[4,16,768]{2,1,0:T(8,128)}), f32[4,16,768]{2,1,0:T(8,128)S(1)}, u32[]{:S(2)}, u32[]{:S(2)}) async-start(f32[4,16,768]{2,1,0:T(8,128)} %fusion.66), calls=%async_computation.3 | async-start | bytes 393216 | tf_op jit(solution)/shard_map/while/body/eval_jaxpr/all_to_all | solution.py:33
  441.1 13.6 %all-to-all-start.1 = ((f32[8,64,192]{2,1,0:T(8,128)}), f32[8,64,192]{2,1,0:T(8,128)S(1)}, u32[]{:S(2)}, u32[]{:S(2)}) async-start(f32[8,64,192]{2,1,0:T(8,128)} %convolution_bitcast_fusion.3), calls=%async_computation.1 | async-start | bytes 1048576 | tf_op jit(solution)/shard_map/while/body/eval_jaxpr/all_to_all | solution.py:33
  456.7 11.0 %all-to-all-start.2 = ((bf16[8,64,192]{2,1,0:T(8,128)(2,1)}), bf16[8,64,192]{2,1,0:T(8,128)(2,1)S(1)}, u32[]{:S(2)}, u32[]{:S(2)}) async-start(bf16[8,64,192]{2,1,0:T(8,128)(2,1)} %broadcast_in_dim.125), calls=%async_computation.2 | async-start | bytes 524288 | tf_op jit(solution)/shard_map/while/body/eval_jaxpr/all_to_all | solution.py:11
  471.2 9.7 %all-to-all-start.3 = ((f32[4,16,768]{2,1,0:T(8,128)}), f32[4,16,768]{2,1,0:T(8,128)S(1)}, u32[]{:S(2)}, u32[]{:S(2)}) async-start(f32[4,16,768]{2,1,0:T(8,128)} %fusion.66), calls=%async_computation.3 | async-start | bytes 393216 | tf_op jit(solution)/shard_map/while/body/eval_jaxpr/all_to_all | solution.py:33
  500.7 13.6 %all-to-all-start.1 = ((f32[8,64,192]{2,1,0:T(8,128)}), f32[8,64,192]{2,1,0:T(8,128)S(1)}, u32[]{:S(2)}, u32[]{:S(2)}) async-start(f32[8,64,192]{2,1,0:T(8,128)} %convolution_bitcast_fusion.3), calls=%async_computation.1 | async-start | bytes 1048576 | tf_op jit(solution)/shard_map/while/body/eval_jaxpr/all_to_all | solution.py:33
  516.3 11.0 %all-to-all-start.2 = ((bf16[8,64,192]{2,1,0:T(8,128)(2,1)}), bf16[8,64,192]{2,1,0:T(8,128)(2,1)S(1)}, u32[]{:S(2)}, u32[]{:S(2)}) async-start(bf16[8,64,192]{2,1,0:T(8,128)(2,1)} %broadcast_in_dim.125), calls=%async_computation.2 | async-start | bytes 524288 | tf_op jit(solution)/shard_map/while/body/eval_jaxpr/all_to_all | solution.py:11
  530.8 9.7 %all-to-all-start.3 = ((f32[4,16,768]{2,1,0:T(8,128)}), f32[4,16,768]{2,1,0:T(8,128)S(1)}, u32[]{:S(2)}, u32[]{:S(2)}) async-start(f32[4,16,768]{2,1,0:T(8,128)} %fusion.66), calls=%async_computation.3 | async-start | bytes 393216 | tf_op jit(solution)/shard_map/while/body/eval_jaxpr/all_to_all | solution.py:33
  541.1 6.7 %collective-permute-start = (bf16[16,768]{1,0:T(8,128)(2,1)S(1)}, bf16[16,768]{1,0:T(8,128)(2,1)S(1)}, u32[]{:S(2)}, u32[]{:S(2)}) collective-permute-start(bf16[16,768]{1,0:T(8,128)(2,1)S(1)} %get-tuple-element.474), channel_id=1, source_target_pairs={{4,0},{8,4},{12,8},{16,12},{20,16},{24,20},{28,24},{5,1},{9,5},{13... | collective-permute-start | bytes 73736 | tf_op jit(solution)/shard_map/while/body/eval_jaxpr/ppermute | solution.py:40
  (45 other events, 704.1 us)
where the time goes:
time: 562 us; the launch traced here: 554 us
  matrix products  148 us (26%)
  starting transfers between devices  142 us (25%)
  waiting for transfers between devices  138 us (25%)
  blocking collectives  86.4 us (15%)
  other arithmetic  18.8 us (3%)
  local copies, waits for them, and re-layouts  17.8 us (3%)
    all_to_all x9, blocking collectives, copy_for_each(): return lax.all_to_all(copies, axis, split_axis=0, concat_axis=0, tiled=True)  86.4 us
    all_to_all x18, waiting for transfers between devices, sum_at_owner(): lax.all_to_all(tiles, axis, split_axis=0, concat_axis=0, tiled=True)  83.9 us
    all_to_all x18, starting transfers between devices, sum_at_owner(): lax.all_to_all(tiles, axis, split_axis=0, concat_axis=0, tiled=True)  77.8 us
    all_to_all x10, waiting for transfers between devices, copy_for_each(): return lax.all_to_all(copies, axis, split_axis=0, concat_axis=0, tiled=True)  54.1 us
    all_to_all x10, starting transfers between devices, copy_for_each(): return lax.all_to_all(copies, axis, split_axis=0, concat_axis=0, tiled=True)  53 us
    dot_general x9, matrix products, tick(): lax.dot_general(input_here, value_grad, (((0,), (0,)), ((), ())), preferr...  46.8 us
    dot_general x9, matrix products, tick(): lax.dot_general(context_here, grad_cols, (((0,), (0,)), ((), ())), prefer...  45.4 us
    dot_general x9, matrix products, tick(): lax.dot_general(value_grad, value_proj, (((1,), (1,)), ((), ())), preferr...  28.5 us
  transfers between devices with their start and end apart: 37, of which 28 were waited for; matrix products, arithmetic and copies ran while one was open for 17% of the time, Pallas kernels for 0%

commit v1 on v0

v1 whole, which is shorter than its diff:
```python
import functools

import jax
import jax.numpy as jnp
from jax import lax
from jax.experimental import pallas as pl
from jax.experimental.pallas import tpu as pltpu
from jax.sharding import PartitionSpec as P

HEAD_DIM = 128
CTX_ROWS = 256
MESH = pl.DeviceIdType.MESH
F32 = jnp.float32
BF16 = jnp.bfloat16


def kernel(
    tokens,
    sections,
    cot, inp, q_hbm, k_hbm, wo_hbm, wv_hbm,
    grad_out, uin_out, vg_out, xin_out,
    wo, wv, q, k, att, cotg, xg, u, csend, crecv, acc, ysend, yrecv, ufin, turned,
    load_sem, own_sem, cs_sem, cr_sem, ys_sem, yr_sem, fs_sem, fr_sem, ag_sem, agr_sem, xs_sem, xr_sem,
):
    head_cols, width = wo.shape
    micro, part, _ = cot.shape
    seq = tokens // micro
    dp = lax.axis_index("dp")
    sec = lax.axis_index("section")
    ten = lax.axis_index("tensor")
    x, z = dp // 2, dp % 2
    dp_peers = ({"dp": x * 2 + (1 - z)}, {"dp": (x + 1 - 2 * (x % 2)) * 2 + z}, {"dp": (3 - x) * 2 + z})
    y_peers = ({"tensor": ten + 1 - 2 * (ten % 2)}, {"tensor": 3 - ten})
    y_all = [{"tensor": (ten + i) % 4} for i in (1, 2, 3)]
    above = {"section": jnp.minimum(sec + 1, sections - 1)}
    below = {"section": jnp.maximum(sec - 1, 0)}
    is_top = sec == sections - 1
    is_bottom = sec == 0

    loads = [
        pltpu.make_async_copy(src, dst, load_sem.at[i])
        for i, (src, dst) in enumerate(((wo_hbm, wo), (q_hbm, q), (k_hbm, k), (wv_hbm, wv)))
    ]
    for load in loads:
        load.start()

    barrier = pltpu.get_barrier_semaphore()
    for peer in (*dp_peers, *y_all):
        pl.semaphore_signal(barrier, inc=1, device_id=peer, device_id_type=MESH)

    @pl.when(jnp.logical_not(is_top))
    def _():
        pl.semaphore_signal(barrier, inc=1, device_id=above, device_id_type=MESH)

    @pl.when(jnp.logical_not(is_bottom))
    def _():
        pl.semaphore_signal(barrier, inc=1, device_id=below, device_id_type=MESH)

    linked = jnp.where(is_top, 0, 1) + jnp.where(is_bottom, 0, 1)
    pl.semaphore_wait(barrier, 6 + linked)

    def own_tokens(ref):
        return ref.at[:, pl.ds(pl.multiple_of(ten * part, part), part), :]

    def gathers(src, dst, send_sem, recv_sem):
        return [
            pltpu.make_async_remote_copy(
                src_ref=src,
                dst_ref=own_tokens(dst),
                send_sem=send_sem.at[i],
                recv_sem=recv_sem.at[i],
                device_id=peer,
                device_id_type=MESH,
            )
            for i, peer in enumerate(y_all)
        ]

    cot_copies = gathers(cot, cotg, ag_sem, agr_sem)
    inp_copies = gathers(inp, xg, xs_sem, xr_sem)

    @pl.when(is_top)
    def _():
        for copy in cot_copies:
            copy.start()
        cotg[:, pl.ds(pl.multiple_of(ten * part, part), part), :] = cot[...]

    heads = head_cols // HEAD_DIM
    loads[1].wait()
    loads[2].wait()
    rows_i = lax.broadcasted_iota(jnp.int32, (tokens, tokens), 0)
    cols_i = lax.broadcasted_iota(jnp.int32, (tokens, tokens), 1)
    allowed = (rows_i >= cols_i) & ((rows_i // seq) == (cols_i // seq))
    for h in range(heads):
        cols = slice(h * HEAD_DIM, (h + 1) * HEAD_DIM)
        q_head = q[:, :, cols].reshape(tokens, HEAD_DIM)
        k_head = k[:, :, cols].reshape(tokens, HEAD_DIM)
        scores = lax.dot_general(q_head, k_head, (((1,), (1,)), ((), ())), preferred_element_type=F32)
        scores = scores / jnp.sqrt(F32(HEAD_DIM))
        scores = jnp.where(allowed, scores, F32(-1e30))
        expo = jnp.exp(scores - jnp.max(scores, axis=-1, keepdims=True))
        att[h] = (expo / jnp.sum(expo, axis=-1, keepdims=True)).astype(BF16)

    n_ctx = head_cols // CTX_ROWS
    n_y = 4
    y_rows = width // n_y

    def forward(e):
        rows = pl.ds(e * y_rows, y_rows)
        return pltpu.make_async_remote_copy(
            src_ref=ufin.at[rows],
            dst_ref=u.at[rows],
            send_sem=fs_sem.at[e],
            recv_sem=fr_sem.at[e],
            device_id=below,
            device_id_type=MESH,
        )

    @pl.when(is_top)
    def _():
        for copy in cot_copies:
            copy.wait_recv()
        whole = cotg[...].reshape(tokens, width).astype(F32)
        u[...] = whole.T.astype(BF16)

    loads[0].wait()

    @pl.when(jnp.logical_not(is_top))
    def _():
        for e in range(n_y):
            forward(e).wait_recv()

    def ctx_copy(step, c):
        rows = pl.ds(c * CTX_ROWS, CTX_ROWS)
        return pltpu.make_async_remote_copy(
            src_ref=csend.at[step, rows],
            dst_ref=crecv.at[step, rows],
            send_sem=cs_sem.at[step, c],
            recv_sem=cr_sem.at[step, c],
            device_id=dp_peers[(c + step) % 3],
            device_id_type=MESH,
        )

    u_here = u[...]
    for c in range(n_ctx):
        rows = pl.ds(c * CTX_ROWS, CTX_ROWS)
        csend[0, rows] = jnp.dot(wo[rows], u_here, preferred_element_type=F32).astype(BF16)
        ctx_copy(0, c).start()

    for copy in inp_copies:
        copy.start()
    xg[:, pl.ds(pl.multiple_of(ten * part, part), part), :] = inp[...]

    for step in (0, 1):
        for c in range(n_ctx):
            rows = pl.ds(c * CTX_ROWS, CTX_ROWS)
            ctx_copy(step, c).wait_recv()
            csend[step + 1, rows] = (csend[step, rows].astype(F32) + crecv[step, rows].astype(F32)).astype(BF16)
            ctx_copy(step + 1, c).start()

    loads[3].wait()

    def y_copy(step, e):
        rows = pl.ds(e * y_rows, y_rows)
        return pltpu.make_async_remote_copy(
            src_ref=ysend.at[step, rows],
            dst_ref=yrecv.at[step, rows],
            send_sem=ys_sem.at[step, e],
            recv_sem=yr_sem.at[step, e],
            device_id=y_peers[(e + step) % 2],
            device_id_type=MESH,
        )

    for c in range(n_ctx):
        rows = pl.ds(c * CTX_ROWS, CTX_ROWS)
        ctx_copy(2, c).wait_recv()
        whole = (csend[2, rows].astype(F32) + crecv[2, rows].astype(F32)).astype(BF16)
        pieces = []
        for i in range(CTX_ROWS // HEAD_DIM):
            head = c * (CTX_ROWS // HEAD_DIM) + i
            pieces.append(
                jnp.dot(
                    whole[i * HEAD_DIM : (i + 1) * HEAD_DIM], att[head], preferred_element_type=F32
                ).astype(BF16)
            )
        value = jnp.concatenate(pieces, axis=0)
        vg_out[rows] = value
        if c < n_ctx - 1:
            term = jnp.dot(wv[:, rows], value, preferred_element_type=F32)
            acc[...] = term + (u[...].astype(F32) * F32(0.25) if c == 0 else acc[...])
        else:
            for e in range(n_y):
                y_part = pl.ds(e * y_rows, y_rows)
                term = jnp.dot(wv[y_part, rows], value, preferred_element_type=F32)
                ysend[0, y_part] = (acc[y_part] + term).astype(BF16)
                y_copy(0, e).start()

    for e in range(n_y):
        y_part = pl.ds(e * y_rows, y_rows)
        y_copy(0, e).wait_recv()
        ysend[1, y_part] = (ysend[0, y_part].astype(F32) + yrecv[0, y_part].astype(F32)).astype(BF16)
        y_copy(1, e).start()

    for e in range(n_y):
        y_part = pl.ds(e * y_rows, y_rows)
        y_copy(1, e).wait_recv()
        ufin[y_part] = (ysend[1, y_part].astype(F32) + yrecv[1, y_part].astype(F32)).astype(BF16)

        @pl.when(jnp.logical_not(is_bottom))
        def _():
            forward(e).start()

    turned[...] = ufin[...].astype(F32).T.astype(BF16)
    for m in range(micro):
        grad_out[m] = turned[pl.ds(pl.multiple_of(m * seq + ten * part, part), part), :]
    uin_out[...] = u[...]
    for copy in inp_copies:
        copy.wait_recv()
    xin_out[...] = xg[...]

    for copy in inp_copies:
        copy.wait_send()
    for step in range(3):
        for c in range(n_ctx):
            ctx_copy(step, c).wait_send()
    for step in range(2):
        for e in range(n_y):
            y_copy(step, e).wait_send()

    @pl.when(is_top)
    def _():
        for copy in cot_copies:
            copy.wait_send()

    @pl.when(jnp.logical_not(is_bottom))
    def _():
        for e in range(n_y):
            forward(e).wait_send()


def per_device(sections, cotangent, inputs, queries, keys, context, value_weight, out_weight):
    micro, part, width = cotangent.shape
    seq, head_cols = queries.shape[2], queries.shape[3]
    tokens = micro * seq
    heads = head_cols // HEAD_DIM
    n_ctx = head_cols // CTX_ROWS
    vmem = pl.BlockSpec(memory_space=pltpu.VMEM)
    anywhere = pl.BlockSpec(memory_space=pl.ANY)
    dma = pltpu.SemaphoreType.DMA
    grads, u_in, vg, x_in = pl.pallas_call(
        functools.partial(kernel, tokens, sections),
        out_shape=(
            jax.ShapeDtypeStruct((micro, part, width), BF16),
            jax.ShapeDtypeStruct((width, tokens), BF16),
            jax.ShapeDtypeStruct((head_cols, tokens), BF16),
            jax.ShapeDtypeStruct((micro, seq, width), BF16),
        ),
        in_specs=[vmem, vmem, anywhere, anywhere, anywhere, anywhere],
        out_specs=(vmem, vmem, vmem, vmem),
        scratch_shapes=[
            pltpu.VMEM((head_cols, width), BF16),
            pltpu.VMEM((width, head_cols), BF16),
            pltpu.VMEM((micro, seq, head_cols), BF16),
            pltpu.VMEM((micro, seq, head_cols), BF16),
            pltpu.VMEM((heads, tokens, tokens), BF16),
            pltpu.VMEM((micro, seq, width), BF16),
            pltpu.VMEM((micro, seq, width), BF16),
            pltpu.VMEM((width, tokens), BF16),
            pltpu.VMEM((3, head_cols, tokens), BF16),
            pltpu.VMEM((3, head_cols, tokens), BF16),
            pltpu.VMEM((width, tokens), F32),
            pltpu.VMEM((2, width, tokens), BF16),
            pltpu.VMEM((2, width, tokens), BF16),
            pltpu.VMEM((width, tokens), BF16),
            pltpu.VMEM((tokens, width), BF16),
            dma((4,)),
            dma((1,)),
            dma((3, n_ctx)),
            dma((3, n_ctx)),
            dma((2, 4)),
            dma((2, 4)),
            dma((4,)),
            dma((4,)),
            dma((3,)),
            dma((3,)),
            dma((3,)),
            dma((3,)),
        ],
        compiler_params=pltpu.CompilerParams(collective_id=0, has_side_effects=True),
    )(cotangent, inputs[0], queries[0], keys[0], out_weight[0], value_weight[0])
    context_flat = context[0].reshape(tokens, head_cols)
    out_grad = lax.dot_general(
        context_flat, u_in, (((0,), (1,)), ((), ())), preferred_element_type=F32
    ).astype(BF16)
    value_grad = lax.dot_general(
        x_in.reshape(tokens, width), vg, (((0,), (1,)), ((), ())), preferred_element_type=F32
    ).astype(BF16)
    return grads[None], value_grad[None], out_grad[None]


def solution(mesh):
    placed = (
        P(None, "tensor", "dp"),
        P("section", None, "tensor", "dp"),
        P("section", None, None, "tensor"),
        P("section", None, None, "tensor"),
        P("section", None, None, "tensor"),
        P("section", "dp", "tensor"),
        P("section", "tensor", "dp"),
    )
    return jax.shard_map(
        functools.partial(per_device, mesh.shape["section"]),
        mesh=mesh,
        in_specs=placed,
        out_specs=(
            P("section", None, "tensor", "dp"),
            P("section", "dp", "tensor"),
            P("section", "tensor", "dp"),
        ),
        check_vma=False,
    )
```

time: 562 us -> 194 us (0.35); the launches traced: 554 us -> 193 us
  Pallas kernels: 0 us -> 184 us
  matrix products: 148 us -> 4.1 us
  starting transfers between devices: 142 us -> 0 us
  waiting for transfers between devices: 138 us -> 0 us
  blocking collectives: 86.4 us -> 0 us
  other arithmetic: 18.8 us -> 0 us
  local copies, waits for them, and re-layouts: 17.8 us -> 4.06 us
    pallas_call x0 -> x1, Pallas kernels: none -> 184 us  [per_device(): pl.pallas_call(functools.partial(kernel, tokens, sections), out_shape=(ja...]
    dot_general x45 -> x2, matrix products: 146 us -> 4.1 us  [the longest x1 3.34 us: per_device(): lax.dot_general(x_in.reshape(tokens, width), vg, (((0,), (1,)), ((), ()))...]
    all_to_all x28 -> x0, waiting for transfers between devices: 138 us -> none  [the longest x18 83.9 us: sum_at_owner(): lax.all_to_all(tiles, axis, split_axis=0, concat_axis=0, tiled=True)]
    all_to_all x28 -> x0, starting transfers between devices: 131 us -> none  [the longest x18 77.8 us: sum_at_owner(): lax.all_to_all(tiles, axis, split_axis=0, concat_axis=0, tiled=True)]
    all_to_all x9 -> x0, blocking collectives: 86.4 us -> none  [copy_for_each(): return lax.all_to_all(copies, axis, split_axis=0, concat_axis=0, tiled=True)]
    ppermute x9 -> x0, starting transfers between devices: 11.5 us -> none  [shifted(): return lax.ppermute(array, axis, pairs)]
    broadcast_in_dim x21 -> x0, local copies, waits for them, and re-layouts: 8.06 us -> none  [the longest x19 8.05 us: copy_for_each(): copies = jnp.broadcast_to(array, (lax.axis_size(axis), *array.shape))]
    select_n x10 -> x0, other arithmetic: 6.83 us -> none  [the longest x9 6.82 us: tick(): incoming = jnp.where(section_place == section_count - 1, cot_here, received)]
  transfers between devices with their start and end apart: 37 -> 0, of which waited for: 28 -> 0; matrix products, arithmetic and copies ran while one was open for 17% -> 0% of each run, Pallas kernels for 0% -> 0%
where the time goes in v1:
time: 194 us; the launch traced here: 193 us
  Pallas kernels  184 us (95%)
  matrix products  4.1 us (2%)
  local copies, waits for them, and re-layouts  4.06 us (2%)
    pallas_call x1, Pallas kernels, per_device(): pl.pallas_call(functools.partial(kernel, tokens, sections), out_shape=(ja...  184 us
    unnamed x8, local copies, waits for them, and re-layouts  4.06 us

profile of v1, /device:TPU:2, one launch (start us, length us, event | category | flops | bytes accessed | tf_op | source)
XLA Modules:
  0.0 193.3 jit_solution(14897593488045785993)
XLA Ops:
  0.6 0.0 copy-start
  0.6 1.0 copy-done
  1.6 184.5 %shard_map.94 = (bf16[2,16,768]{2,1,0:T(8,128)(2,1)}, bf16[768,128]{1,0:T(8,128)(2,1)}, bf16[1536,128]{1,0:T(8,128)(2,1)}, bf16[2,64,768]{2,1,0:T(8,128)(2,1)}) custom-call(bf16[2,16,768]{2,1,0:T(8,128)(2,1)} %cot.1, bf16[2,16,768]{2,1,0:T(8,128)(2,1)} %bitcast.24, bf16[2,64,1536]{2,1,0:T(8,128)(2,1)} %bitcast.21, bf16[2,64,1536]{2,1,0:T(8,128)(2,1)} %bitcast.22, ...), custom_call_target="tpu_custom_call" | custom-call | tf_op jit(solution)/shard_map/pallas_call | solution.py:249
  186.1 0.0 copy-start.1
  186.1 3.3 %fusion = bf16[1,768,1536]{2,1,0:T(8,128)(2,1)} fusion(bf16[128,768]{1,0:T(8,128)(2,1)} %bitcast.23, bf16[1536,128]{1,0:T(8,128)(2,1)} %get-tuple-element.9), kind=kOutput, calls=%fused_computation.2 | convolution fusion | flops 303169536 | bytes 2949120 | tf_op jit(solution)/shard_map/dot_general | solution.py:294
  189.5 0.0 copy-done.1
  189.5 0.8 fusion.1
  190.2 0.0 copy-start.2
  190.2 2.4 %copy.10 = bf16[1,1536,768]{2,1,0:T(8,128)(2,1)} copy(bf16[1,1536,768]{1,2,0:T(8,128)(2,1)S(1)} %fusion.1) | data formatting | bytes 4718592
  192.7 0.0 copy-done.2
  192.7 0.6 copy.12
Async XLA Ops:
  0.6 1.0 copy-start
  186.1 3.4 %copy-start.1 = (bf16[768,128]{1,0:T(8,128)(2,1)S(1)}, bf16[768,128]{1,0:T(8,128)(2,1)}, u32[]{:S(2)}) copy-start(bf16[768,128]{1,0:T(8,128)(2,1)} %get-tuple-element.10) | copy-start | bytes 589828
  190.2 2.4 %copy-start.2 = (bf16[2,16,768]{2,1,0:T(8,128)(2,1)S(1)}, bf16[2,16,768]{2,1,0:T(8,128)(2,1)}, u32[]{:S(2)}) copy-start(bf16[2,16,768]{2,1,0:T(8,128)(2,1)} %get-tuple-element.7) | copy-start | bytes 147460
